TPU v7x, 32 devices: a whole 2x2x4 slice. The times are simulated.
32 devices in a mesh: replica: 4 (over y, core), shard: 8 (over z, x).
Axes of the slice: x: 2, y: 2, z: 4, core: 2. Of those that a mesh axis runs over, the one named last changes fastest.
Arguments:
- anchor: float32 [384, 8192], P('shard'), may hold values from -6 to 6
- replica_rows: bfloat16 [4, 384, 8192], P('replica', 'shard'), may hold values from -6 to 6
- outer_velocity: float32 [384, 8192], P('shard', 'replica'), may hold values from -6 to 6
- features: bfloat16 [4, 384, 256], P('replica', 'shard'), may hold values from -6 to 6
- cotangent: bfloat16 [4, 256, 1024], P('replica', 'shard'), may hold values from -0.375 to 0.375
- inner_weight: float32 [4, 384, 1024], P('replica', 'shard'), may hold values from -6 to 6
- first_moment: float32 [4, 384, 1024], P('replica', 'shard'), may hold values from -6 to 6
- second_moment: float32 [4, 384, 1024], P('replica', 'shard'), may hold values from 0.5 to 2
Outputs:
- new_anchor: float32 [384, 8192], P('shard')
- merged_rows: bfloat16 [4, 384, 8192], P('replica', 'shard')
- new_velocity: float32 [384, 8192], P('shard', 'replica')
- new_weight: float32 [4, 384, 1024], P('replica', 'shard')
- new_first: float32 [4, 384, 1024], P('replica', 'shard')
- new_second: float32 [4, 384, 1024], P('replica', 'shard')
All inputs are finite; a program needn't handle non-finite values.
Results may differ from a plain program's by a relative error of at most 0.0035.
Values may be sent and summed in bfloat16 or wider, within the bound.
A program may use at most 64 MiB of HBM per device.

v0:
```python
import jax
import jax.numpy as jnp
from jax import lax
from jax.sharding import PartitionSpec as P

momentum_keep = 0.9
outer_rate = 0.7
blend_keep = 0.5
inner_rate = 0.01
decay_first = 0.9
decay_second = 0.95
weight_decay = 0.1
epsilon = 1e-08
first_fix = 1.0 - 0.9**10
second_fix = 1.0 - 0.95**10


def outer_sync(anchor, replica_rows, outer_velocity):
    replicas = lax.axis_size("replica")
    own_rows = replica_rows[0].astype(jnp.float32)
    slice_width = outer_velocity.shape[1]
    offset = lax.axis_index("replica") * slice_width
    drift = anchor - own_rows
    summed = lax.psum(drift, "replica")
    velocity_all = lax.all_gather(
        outer_velocity.astype(jnp.bfloat16), "replica", axis=1, tiled=True
    ).astype(outer_velocity.dtype)
    outer_grad = summed / replicas
    velocity_next = momentum_keep * velocity_all + outer_grad
    new_anchor = anchor - outer_rate * (outer_grad + momentum_keep * velocity_next)
    new_velocity = lax.dynamic_slice_in_dim(velocity_next, offset, slice_width, 1)
    merged_rows = (blend_keep * own_rows + (1.0 - blend_keep) * new_anchor).astype(jnp.bfloat16)
    return (new_anchor, merged_rows[None], new_velocity)


def inner_update(features, cotangent, inner_weight, first_moment, second_moment):
    feature_rows = features[0]
    gradient = jnp.dot(
        feature_rows,
        lax.all_gather(cotangent, "shard", axis=1, tiled=True)[0],
        preferred_element_type=jnp.float32,
    )[None]
    new_first = decay_first * first_moment + (1.0 - decay_first) * gradient
    new_second = decay_second * second_moment + (1.0 - decay_second) * gradient * gradient
    stepped = new_first / first_fix / (jnp.sqrt(new_second / second_fix) + epsilon)
    new_weight = inner_weight - inner_rate * (stepped + weight_decay * inner_weight)
    return (new_weight, new_first, new_second)


def local(
    anchor,
    replica_rows,
    outer_velocity,
    features,
    cotangent,
    inner_weight,
    first_moment,
    second_moment,
):
    new_weight, new_first, new_second = inner_update(
        features, cotangent, inner_weight, first_moment, second_moment
    )
    new_anchor, merged_rows, new_velocity = outer_sync(anchor, replica_rows, outer_velocity)
    return (new_anchor, merged_rows, new_velocity, new_weight, new_first, new_second)


def solution(mesh):
    in_specs = (
        P("shard", None),
        P("replica", "shard", None),
        P("shard", "replica"),
        P("replica", "shard", None),
        P("replica", "shard", None),
        P("replica", "shard", None),
        P("replica", "shard", None),
        P("replica", "shard", None),
    )
    out_specs = (
        P("shard", None),
        P("replica", "shard", None),
        P("shard", "replica"),
        P("replica", "shard", None),
        P("replica", "shard", None),
        P("replica", "shard", None),
    )
    return jax.shard_map(local, mesh=mesh, in_specs=in_specs, out_specs=out_specs, check_vma=False)
```

profile of v0, /device:TPU:0, one launch (start us, length us, event | category | flops | bytes accessed | tf_op | source)
XLA Modules:
  0.0 71.8 jit_solution(1049866319276950009)
XLA Ops:
  7.2 0.0 copy-start
  7.2 0.0 all-reduce.2.cloned.1.call-start
  7.2 2.9 %convert_subtract_fusion = f32[48,8192]{1,0:T(8,128)} fusion(f32[48,8192]{1,0:T(8,128)} %param.8, bf16[1,48,8192]{2,1,0:T(8,128)(2,1)} %param.9), kind=kLoop, calls=%fused_computation.1 | loop fusion | flops 786432 | bytes 3932160 | tf_op jit(solution)/shard_map/sub | solution.py:23
  10.1 0.0 copy-start.7
  10.1 0.0 copy-start.4
  10.1 0.0 copy-start.5
  10.1 0.0 copy-start.6
  10.1 0.0 all-reduce.2.cloned.1.call-update
  10.2 0.9 %copy-done.3 = f32[48,2048]{1,0:T(8,128)S(1)} copy-done((f32[48,2048]{1,0:T(8,128)S(1)}, f32[48,2048]{1,0:T(8,128)}, u32[]{:S(2)}) %copy-start.3) | copy-done | bytes 393240
  11.1 0.0 copy-done.7
  11.1 0.0 copy-start.1
  11.2 0.0 copy-start.2
  11.2 33.3 %all_gather.7 = bf16[1,256,1024]{2,1,0:T(8,128)(2,1)S(1)} all-gather(bf16[1,32,1024]{2,1,0:T(8,128)(2,1)S(1)} %copy-done.7), channel_id=1, replica_groups=mesh['replica'=4,'shard'=8] {'shard'}, dimensions={1}, use_global_device_ids=true | all-gather | bytes 589824 | tf_op jit(solution)/shard_map/all_gather | solution.py:40
  44.4 0.0 copy-done
  44.4 0.0 copy-done.4
  44.4 0.0 copy-done.5
  44.5 0.0 copy-done.6
  44.5 1.1 %multiply_subtract_fusion.1 = (f32[1,48,1024]{2,1,0:T(8,128)}, f32[1,48,1024]{2,1,0:T(8,128)}, f32[1,48,1024]{2,1,0:T(8,128)}) fusion(f32[1,48,1024]{2,1,0:T(8,128)S(1)} %copy-done.4, f32[1,48,1024]{2,1,0:T(8,128)S(1)} %copy-done.5, f32[1,48,1024]{2,1,0:T(8,128)S(1)} %copy-done.6, bf16[1,256,1024]{2,1,0:T(8,128)(2,1)S(1)} %all_gather.7, ...), kind=kOutput, calls=%fused_computation.13 | convolution fusion | flops 25903104 | bytes 1728512 | tf_op jit(solution)/shard_map/dot_general | solution.py:38
  45.6 13.3 %all_gather.6 = bf16[48,8192]{1,0:T(8,128)(2,1)S(1)} all-gather(bf16[48,2048]{1,0:T(8,128)(2,1)S(1)} %convert_element_type.17), channel_id=1, replica_groups=mesh['replica'=4,'shard'=8] {'replica'}, dimensions={1}, use_global_device_ids=true | all-gather | bytes 983040 | tf_op jit(solution)/shard_map/all_gather | solution.py:25
  58.9 1.9 %all-reduce.2.cloned.1.call-done = f32[48,8192]{1,0:T(8,128)} async-done(((f32[48,8192]{1,0:T(8,128)}), f32[48,8192]{1,0:T(8,128)}) %all-reduce.2.cloned.1.call-update) | async-done | bytes 1572880 | tf_op jit(solution)/shard_map/psum | solution.py:24
  60.8 0.0 copy-done.1
  60.8 0.0 copy-done.2
  60.8 3.4 %fusion.2 = (bf16[1,48,8192]{2,1,0:T(8,128)(2,1)}, f32[48,8192]{1,0:T(8,128)}, f32[48,8192]{1,0:T(8,128)S(1)}) fusion(bf16[1,48,8192]{2,1,0:T(8,128)(2,1)S(1)} %copy-done.2, f32[48,8192]{1,0:T(8,128)S(1)} %copy-done.1, bf16[48,8192]{1,0:T(8,128)(2,1)S(1)} %all_gather.6, f32[48,8192]{1,0:T(8,128)} %all-reduce.2.cloned.1.call-done), kind=kLoop, calls=%fused_computation.6 | loop fusion | flops 4718592 | bytes 8650752 | tf_op jit(solution)/shard_map/broadcast_in_dim | solution.py:33
  64.2 0.8 %constant_dynamic-slice_fusion = f32[48,2048]{1,0:T(8,128)} fusion(f32[48,8192]{1,0:T(8,128)S(1)} %get-tuple-element.11, s32[]{:T(128)S(6)} %select_n.3), kind=kLoop, calls=%fused_computation.15 | loop fusion | bytes 786436 | tf_op jit(solution)/shard_map/dynamic_slice | solution.py:31
  (2 shorter events, 0.0 us)
Async XLA Ops:
  7.2 37.3 %copy-start = (bf16[1,48,256]{2,1,0:T(8,128)(2,1)S(1)}, bf16[1,48,256]{2,1,0:T(8,128)(2,1)}, u32[]{:S(2)}) copy-start(bf16[1,48,256]{2,1,0:T(8,128)(2,1)} %param.11) | copy-start | bytes 73732
  7.2 53.6 %all-reduce.2.cloned.1.call-start = ((), (), s32[]{:S(2)}) async-start(), calls=%async_computation | async-start | bytes 3145728 | tf_op jit(solution)/shard_map/psum | solution.py:24
  10.1 1.0 %copy-start.3 = (f32[48,2048]{1,0:T(8,128)S(1)}, f32[48,2048]{1,0:T(8,128)}, u32[]{:S(2)}) copy-start(f32[48,2048]{1,0:T(8,128)} %param.10) | copy-start | bytes 1179652
  10.1 1.0 %copy-start.7 = (bf16[1,32,1024]{2,1,0:T(8,128)(2,1)S(1)}, bf16[1,32,1024]{2,1,0:T(8,128)(2,1)}, u32[]{:S(2)}) copy-start(bf16[1,32,1024]{2,1,0:T(8,128)(2,1)} %param.12) | copy-start | bytes 196612
  10.1 34.3 %copy-start.4 = (f32[1,48,1024]{2,1,0:T(8,128)S(1)}, f32[1,48,1024]{2,1,0:T(8,128)}, u32[]{:S(2)}) copy-start(f32[1,48,1024]{2,1,0:T(8,128)} %param.13) | copy-start | bytes 589828
  10.1 34.3 %copy-start.5 = (f32[1,48,1024]{2,1,0:T(8,128)S(1)}, f32[1,48,1024]{2,1,0:T(8,128)}, u32[]{:S(2)}) copy-start(f32[1,48,1024]{2,1,0:T(8,128)} %param.14) | copy-start | bytes 589828
  10.1 34.3 %copy-start.6 = (f32[1,48,1024]{2,1,0:T(8,128)S(1)}, f32[1,48,1024]{2,1,0:T(8,128)}, u32[]{:S(2)}) copy-start(f32[1,48,1024]{2,1,0:T(8,128)} %param.15) | copy-start | bytes 589828
  11.1 49.6 %copy-start.1 = (f32[48,8192]{1,0:T(8,128)S(1)}, f32[48,8192]{1,0:T(8,128)}, u32[]{:S(2)}) copy-start(f32[48,8192]{1,0:T(8,128)} %param.8) | copy-start | bytes 4718596
  11.2 49.6 %copy-start.2 = (bf16[1,48,8192]{2,1,0:T(8,128)(2,1)S(1)}, bf16[1,48,8192]{2,1,0:T(8,128)(2,1)}, u32[]{:S(2)}) copy-start(bf16[1,48,8192]{2,1,0:T(8,128)(2,1)} %param.9) | copy-start | bytes 2359300
Sparse Core Ops, SparseCore 0:
  10.9 49.7 all-reduce.1
where the time goes:
time: 72 us; the launch traced here: 71.8 us
  blocking collectives  46.6 us (65%)
  between operations  14.1 us (20%)
  other arithmetic  6.34 us (9%)
  waiting for transfers between devices  1.87 us (3%)
  local copies, waits for them, and re-layouts  1.75 us (2%)
  matrix products  1.11 us (2%)
    all_gather x1, blocking collectives, inner_update(): lax.all_gather(cotangent, 'shard', axis=1, tiled=True)[0]  33.3 us
    all_gather x1, blocking collectives, outer_sync(): lax.all_gather(outer_velocity.astype(jnp.bfloat16), 'replica', axis=1, ti...  13.3 us
    broadcast_in_dim x1, other arithmetic, outer_sync(): return (new_anchor, merged_rows[None], new_velocity)  3.43 us
    sub x1, other arithmetic, outer_sync(): drift = anchor - own_rows  2.88 us
    psum x1, waiting for transfers between devices, outer_sync(): summed = lax.psum(drift, 'replica')  1.86 us
  transfers between devices with their start and end apart: 1, of which 1 were waited for; matrix products, arithmetic and copies ran while one was open for 2% of the time, Pallas kernels for 0%

commit v1 on v0

--- a/solution.py
+++ b/solution.py
@@ -2,6 +2,7 @@
 import jax.numpy as jnp
 from jax import lax
 from jax.sharding import PartitionSpec as P
+from jax.lax import all_gather
 
 momentum_keep = 0.9
 outer_rate = 0.7
@@ -22,8 +23,8 @@
     offset = lax.axis_index("replica") * slice_width
     drift = anchor - own_rows
     summed = lax.psum(drift, "replica")
-    velocity_all = lax.all_gather(
-        outer_velocity.astype(jnp.bfloat16), "replica", axis=1, tiled=True
+    velocity_all = jnp.concatenate(
+        all_gather(outer_velocity.astype(jnp.bfloat16), "replica"), axis=1
     ).astype(outer_velocity.dtype)
     outer_grad = summed / replicas
     velocity_next = momentum_keep * velocity_all + outer_grad

time: 72 us -> 69.1 us (0.960)
  blocking collectives: 46.6 us -> 42.1 us
  local copies, waits for them, and re-layouts: 1.75 us -> 3.68 us
  waiting for transfers between devices: 1.87 us -> 0.02 us
  matrix products: 1.11 us -> 2.13 us
    all_gather x1, blocking collectives: 13.3 us -> 10.1 us  [outer_sync(): all_gather(outer_velocity.astype(jnp.bfloat16), 'replica')]
    psum x1, waiting for transfers between devices: 1.86 us -> 0.01 us  [outer_sync(): summed = lax.psum(drift, 'replica')]
    all_gather x1, blocking collectives: 33.3 us -> 32 us  [inner_update(): lax.all_gather(cotangent, 'shard', axis=1, tiled=True)[0]]
    dot_general x1, matrix products: 1.11 us -> 2.13 us  [inner_update(): jnp.dot(feature_rows, lax.all_gather(cotangent, 'shard', axis=1, tiled=Tr...]
    mul x0 -> x1, local copies, waits for them, and re-layouts: none -> 1.01 us  [outer_sync(): velocity_next = momentum_keep * velocity_all + outer_grad]
    unnamed x16 -> x11, local copies, waits for them, and re-layouts: 0.98 us -> 1.9 us
  transfers between devices with their start and end apart: 1 -> 1, of which waited for: 1 -> 0; matrix products, arithmetic and copies ran while one was open for 2% -> 6% of each run, Pallas kernels for 0% -> 0%
where the time goes in v1:
time: 69.1 us; the launch traced here: 68.8 us
  blocking collectives  42.1 us (61%)
  between operations  14.1 us (20%)
  other arithmetic  6.73 us (10%)
  local copies, waits for them, and re-layouts  3.68 us (5%)
  matrix products  2.13 us (3%)
    all_gather x1, blocking collectives, inner_update(): lax.all_gather(cotangent, 'shard', axis=1, tiled=True)[0]  32 us
    all_gather x1, blocking collectives, outer_sync(): all_gather(outer_velocity.astype(jnp.bfloat16), 'replica')  10.1 us
    broadcast_in_dim x1, other arithmetic, outer_sync(): return (new_anchor, merged_rows[None], new_velocity)  3.65 us
    sub x1, other arithmetic, outer_sync(): drift = anchor - own_rows  2.88 us
    dot_general x1, matrix products, inner_update(): jnp.dot(feature_rows, lax.all_gather(cotangent, 'shard', axis=1, tiled=Tr...  2.13 us
    unnamed x11, local copies, waits for them, and re-layouts  1.9 us
  transfers between devices with their start and end apart: 1, of which 0 were waited for; matrix products, arithmetic and copies ran while one was open for 6% of the time, Pallas kernels for 0%

profile of v1, /device:TPU:0, one launch (start us, length us, event | category | flops | bytes accessed | tf_op | source)
XLA Modules:
  0.0 68.8 jit_solution(16332375424898994133)
XLA Ops:
  7.2 0.0 copy-start
  7.2 0.0 all-reduce.2.cloned.1.call-start
  7.2 2.9 %convert_subtract_fusion = f32[48,8192]{1,0:T(8,128)} fusion(f32[48,8192]{1,0:T(8,128)} %param.8, bf16[1,48,8192]{2,1,0:T(8,128)(2,1)} %param.9), kind=kLoop, calls=%fused_computation.1 | loop fusion | flops 786432 | bytes 3932160 | tf_op jit(solution)/shard_map/sub | solution.py:24
  10.1 0.0 copy-start.2
  10.1 0.0 all-reduce.2.cloned.1.call-update
  10.1 1.0 %copy-done.2 = f32[48,2048]{1,0:T(8,128)S(1)} copy-done((f32[48,2048]{1,0:T(8,128)S(1)}, f32[48,2048]{1,0:T(8,128)}, u32[]{:S(2)}) %copy-start.2) | copy-done | bytes 393240
  11.1 10.1 %all-gather = bf16[192,2048]{1,0:T(8,128)(2,1)S(1)} all-gather(bf16[48,2048]{1,0:T(8,128)(2,1)S(1)} %convert_element_type.19), channel_id=2, replica_groups=mesh['replica'=4,'shard'=8] {'replica'}, dimensions={0}, use_global_device_ids=true | all-gather | bytes 983040 | tf_op jit(solution)/shard_map/all_gather | solution.py:27
  21.2 0.2 convert_multiply_fusion
  21.4 1.0 %copy.14 = f32[4,48,2048]{2,0,1:T(4,128)S(1)} copy(f32[4,48,2048]{2,1,0:T(8,128)S(1)} %bitcast.29) | data formatting | bytes 3145728 | tf_op jit(solution)/shard_map/mul | solution.py:30
  22.4 0.0 copy-start.4
  22.5 0.0 copy-start.3
  22.5 0.9 %copy.15 = f32[6,8,4,2048]{3,1,2,0:T(8,128)S(1)} copy(f32[6,8,4,2048]{3,2,1,0:T(4,128)S(1)} %bitcast.30) | data formatting | bytes 3145728
  23.4 0.0 copy-start.1
  23.4 0.0 copy-done.4
  23.4 32.0 %all_gather.11 = bf16[1,256,1024]{2,1,0:T(8,128)(2,1)S(1)} all-gather(bf16[1,32,1024]{2,1,0:T(8,128)(2,1)S(1)} %copy-done.4), channel_id=1, replica_groups=mesh['replica'=4,'shard'=8] {'shard'}, dimensions={1}, use_global_device_ids=true | all-gather | bytes 589824 | tf_op jit(solution)/shard_map/all_gather | solution.py:41
  55.4 0.0 copy-done
  55.4 0.0 copy-done.3
  55.4 2.1 %multiply_subtract_fusion.1 = (f32[1,48,1024]{2,1,0:T(8,128)}, f32[1,48,1024]{2,1,0:T(8,128)}, f32[1,48,1024]{2,1,0:T(8,128)}) fusion(f32[1,48,1024]{2,1,0:T(8,128)S(1)} %copy-done.3, f32[1,48,1024]{2,1,0:T(8,128)} %param.14, f32[1,48,1024]{2,1,0:T(8,128)} %param.15, bf16[1,256,1024]{2,1,0:T(8,128)(2,1)S(1)} %all_gather.11, bf16[1,48,256]{2,1,0:T(8,128)(2,1)S(1)} %copy-done), kind=kOutput, calls=%fused_computation.14 | convolution fusion | flops 25903104 | bytes 1728512 | tf_op jit(solution)/shard_map/dot_general | solution.py:39
  57.5 0.0 all-reduce.2.cloned.1.call-done
  57.5 0.0 copy-done.1
  57.5 3.6 %fusion.2 = (bf16[1,48,8192]{2,1,0:T(8,128)(2,1)}, f32[48,8192]{1,0:T(8,128)}, f32[48,8192]{1,0:T(8,128)S(1)}) fusion(bf16[1,48,8192]{2,1,0:T(8,128)(2,1)} %param.9, f32[48,8192]{1,0:T(8,128)S(1)} %copy-done.1, f32[48,8192]{1,0:T(8,128)S(1)} %bitcast.28, f32[48,8192]{1,0:T(8,128)} %all-reduce.2.cloned.1.call-done), kind=kLoop, calls=%fused_computation.7 | loop fusion | flops 3932160 | bytes 9437184 | tf_op jit(solution)/shard_map/broadcast_in_dim | solution.py:34
  61.2 0.8 %constant_dynamic-slice_fusion = f32[48,2048]{1,0:T(8,128)} fusion(f32[48,8192]{1,0:T(8,128)S(1)} %get-tuple-element.11, s32[]{:T(128)S(6)} %select_n.3), kind=kLoop, calls=%fused_computation.16 | loop fusion | bytes 786436 | tf_op jit(solution)/shard_map/dynamic_slice | solution.py:32
  (1 shorter events, 0.0 us)
Async XLA Ops:
  7.2 48.2 %copy-start = (bf16[1,48,256]{2,1,0:T(8,128)(2,1)S(1)}, bf16[1,48,256]{2,1,0:T(8,128)(2,1)}, u32[]{:S(2)}) copy-start(bf16[1,48,256]{2,1,0:T(8,128)(2,1)} %param.11) | copy-start | bytes 73732
  7.2 50.4 %all-reduce.2.cloned.1.call-start = ((), (), s32[]{:S(2)}) async-start(), calls=%async_computation | async-start | bytes 3145728 | tf_op jit(solution)/shard_map/psum | solution.py:25
  10.1 1.0 %copy-start.2 = (f32[48,2048]{1,0:T(8,128)S(1)}, f32[48,2048]{1,0:T(8,128)}, u32[]{:S(2)}) copy-start(f32[48,2048]{1,0:T(8,128)} %param.10) | copy-start | bytes 1179652
  22.4 1.0 %copy-start.4 = (bf16[1,32,1024]{2,1,0:T(8,128)(2,1)S(1)}, bf16[1,32,1024]{2,1,0:T(8,128)(2,1)}, u32[]{:S(2)}) copy-start(bf16[1,32,1024]{2,1,0:T(8,128)(2,1)} %param.12) | copy-start | bytes 196612
  22.5 33.0 %copy-start.3 = (f32[1,48,1024]{2,1,0:T(8,128)S(1)}, f32[1,48,1024]{2,1,0:T(8,128)}, u32[]{:S(2)}) copy-start(f32[1,48,1024]{2,1,0:T(8,128)} %param.13) | copy-start | bytes 589828
  23.4 34.2 %copy-start.1 = (f32[48,8192]{1,0:T(8,128)S(1)}, f32[48,8192]{1,0:T(8,128)}, u32[]{:S(2)}) copy-start(f32[48,8192]{1,0:T(8,128)} %param.8) | copy-start | bytes 4718596
Sparse Core Ops, SparseCore 0:
  10.9 45.6 all-reduce.1
